TPU v7x, 32 devices: a whole 2x2x4 slice. The times are simulated.
32 devices in a mesh: grp: 2 (over y), slab: 4 (over z), orb: 2 (over x), rep: 2 (over core).
Axes of the slice: x: 2, y: 2, z: 4, core: 2. Of those that a mesh axis runs over, the one named last changes fastest.
Arguments:
- orbitals: bfloat16 [16, 32, 1024], P(('grp', 'slab', 'orb')), parts along dimension 0, may hold values from -6 to 6
- corners: int32 [16, 3], P('grp'), parts along dimension 0, may hold values from 0 to 191, as said below
- partners: int32 [16, 24], P(('grp', 'slab', 'orb')), parts along dimension 0, may hold values from -1 to 7, as said below
- kernel: float32 [32, 1024], replicated, may hold values from 0.05 to 5
Outputs:
- exchange_boxes: float32 [16, 32, 1024], P(('grp', 'slab', 'orb')), parts along dimension 0
- exchange_energy: float32 [2], P('grp'), parts along dimension 0
There are 2 independent parts, one for each index of `grp`. A program takes and returns all parts, laid end to end along the dimension named above; an argument that names none is the same for every part. Nothing has to cross between parts.
Inputs may be any that keep to these rules, and one draw needn't show every extreme that they name: corners[i, 2] lies in the slab of orbital i: from 12 * (i // (1 * 2)) to 12 more less one; corners[i, 0] and corners[i, 1] lie below 192. `partners`: row i starts with i itself, names distinct orbitals whose boxes intersect box i (every component of o is above -32 and below 32), and has its -1 entries only after all others.
All inputs are finite; a program needn't handle non-finite values.
Results may differ from a plain program's by a relative error of at most 0.0003.
Values may be sent and summed in bfloat16 or wider, within the bound.
A program may use at most 64 MiB of HBM per device.

v0:
```python
import math

import jax
import jax.numpy as jnp
from jax import lax
from jax.sharding import PartitionSpec as P

G = 192
ZDEV = 12
PB = 4


def passed_along(array, axis, by):
    size = lax.axis_size(axis)
    return lax.ppermute(array, axis, [(i, (i + by) % size) for i in range(size)])


def wrapped(deltas, lengths):
    halfway = lengths // 2
    return jnp.mod(deltas + halfway, lengths) - halfway


def edge_shifter(offsets, box_edge):
    row_ids = lax.broadcasted_iota(jnp.int32, (offsets.shape[0], box_edge, box_edge), 1)
    col_ids = lax.broadcasted_iota(jnp.int32, (offsets.shape[0], box_edge, box_edge), 2)
    return (col_ids == row_ids + offsets[:, None, None]).astype(jnp.bfloat16)


def plane_shifter(offsets_b, offsets_c, box_edge):
    plane = box_edge * box_edge
    source = lax.broadcasted_iota(jnp.int32, (offsets_b.shape[0], plane, plane), 1)
    target = lax.broadcasted_iota(jnp.int32, (offsets_b.shape[0], plane, plane), 2)
    match_b = source // box_edge == target // box_edge + offsets_b[:, None, None]
    match_c = jnp.mod(source, box_edge) == jnp.mod(target, box_edge) + offsets_c[:, None, None]
    return (match_b & match_c).astype(jnp.bfloat16)


def place_boxes(orbital_boxes, offsets, box_edge):
    stride_along_first = edge_shifter(offsets[:, 0], box_edge)
    displaced_density = jnp.einsum(
        "rkd,rdw->rkw", stride_along_first, orbital_boxes, preferred_element_type=jnp.float32
    ).astype(jnp.bfloat16)
    step_plane = plane_shifter(offsets[:, 1], offsets[:, 2], box_edge)
    return jnp.einsum(
        "pam,pmn->pan", displaced_density, step_plane, preferred_element_type=jnp.float32
    )


def fourier_tables(box_edge):
    grid_ids = jnp.arange(box_edge, dtype=jnp.int32)
    phases = jnp.mod(grid_ids[:, None] * grid_ids[None, :], box_edge)
    angles = phases.astype(jnp.float32) * (2.0 * math.pi / box_edge)
    plane_ids = jnp.arange(box_edge * box_edge, dtype=jnp.int32)
    outer_ids = plane_ids // box_edge
    inner_ids = jnp.mod(plane_ids, box_edge)
    plane_phases = jnp.mod(
        outer_ids[:, None] * outer_ids[None, :] + inner_ids[:, None] * inner_ids[None, :], box_edge
    )
    plane_angles = plane_phases.astype(jnp.float32) * (2.0 * math.pi / box_edge)
    return (jnp.cos(angles), jnp.sin(angles), jnp.cos(plane_angles), jnp.sin(plane_angles))


def edge_rotation(values, matrix):
    return jnp.einsum("ka,pam->pkm", matrix, values, precision=lax.Precision.HIGHEST)


def plane_turn(values, table):
    return jnp.einsum("pam,mn->pan", values, table, precision=lax.Precision.HIGHEST)


def poisson(density, kernel, tables):
    cosine, sine, plane_cos, plane_sin = tables
    plane_real = plane_turn(density, plane_cos)
    plane_imag = -plane_turn(density, plane_sin)
    real_part = edge_rotation(plane_real, cosine) + edge_rotation(plane_imag, sine)
    imag_part = edge_rotation(plane_imag, cosine) - edge_rotation(plane_real, sine)
    real_part = real_part * kernel[None]
    imag_part = imag_part * kernel[None]
    back_real = edge_rotation(real_part, cosine) - edge_rotation(imag_part, sine)
    back_imag = edge_rotation(imag_part, cosine) + edge_rotation(real_part, sine)
    result = plane_turn(back_real, plane_cos) - plane_turn(back_imag, plane_sin)
    box_edge = density.shape[1]
    return result / float(box_edge**3)


def body(orbitals, corners, partners, kernel):
    own_count = orbitals.shape[0]
    box_edge = orbitals.shape[1]
    plane = box_edge * box_edge
    slab_count = lax.axis_size("slab")
    orb_count = lax.axis_size("orb")
    group_size = own_count * orb_count
    slab_position = lax.axis_index("slab")
    halo_depth = (ZDEV + box_edge - 2) // ZDEV
    gathered = lax.all_gather(orbitals, "orb", axis=0, tiled=True)
    lower = [gathered]
    upper = [gathered]
    for _ in range(halo_depth):
        lower.append(passed_along(lower[-1], "slab", 1))
        upper.append(passed_along(upper[-1], "slab", -1))
    nearby = jnp.concatenate(lower[::-1] + upper[1:], axis=0)
    rep_count = lax.axis_size("rep")
    rep_index = lax.axis_index("rep")
    half_slots = partners.shape[1] // rep_count
    chosen = lax.dynamic_index_in_dim(
        partners.reshape(own_count, half_slots, rep_count), rep_index, 2, keepdims=False
    )
    first_own = (slab_position * orb_count + lax.axis_index("orb")) * own_count
    owner_ids = jnp.repeat(jnp.arange(own_count, dtype=jnp.int32), half_slots)
    flat_ids = chosen.reshape(own_count * half_slots)
    usable = (flat_ids >= 0).astype(jnp.float32)
    safe_ids = jnp.maximum(flat_ids, 0)
    neighbour_slab = safe_ids // group_size
    slab_step = jnp.mod(neighbour_slab - slab_position + halo_depth, slab_count) - halo_depth
    pool_rows = (slab_step + halo_depth) * group_size + jnp.mod(safe_ids, group_size)
    lengths = jnp.array([G, G, ZDEV * slab_count], jnp.int32)
    own_corners = jnp.take(corners, first_own + owner_ids, axis=0, mode="clip")
    partner_corners = jnp.take(corners, safe_ids, axis=0, mode="clip")
    offsets = wrapped(own_corners - partner_corners, lengths)
    tables = fourier_tables(box_edge)
    block_size = PB
    block_count = own_count * half_slots // block_size

    def block_work(block_index, carry):
        exchange, energy = carry
        first_pair = block_index * block_size
        owner_slot = first_pair // half_slots
        slots = lax.dynamic_slice_in_dim(pool_rows, first_pair, block_size)
        block_offsets = lax.dynamic_slice_in_dim(offsets, first_pair, block_size, 0)
        block_usable = lax.dynamic_slice_in_dim(usable, first_pair, block_size)

        def active(anchor):
            orbital_boxes = jnp.take(nearby, slots, axis=0, mode="clip")
            shifted = (
                place_boxes(orbital_boxes, block_offsets, box_edge) * block_usable[:, None, None]
            )
            centre = lax.dynamic_index_in_dim(orbitals, owner_slot, 0, keepdims=False).astype(
                jnp.float32
            )
            density = centre[None] * shifted
            potential = poisson(density, kernel, tables)
            return (jnp.sum(potential * shifted, axis=0), jnp.sum(density * potential))

        def skipped(anchor):
            return (jnp.zeros((box_edge, plane), jnp.float32), jnp.zeros((), jnp.float32))

        pair_term, energy_part = lax.cond(jnp.sum(block_usable) > 0.0, active, skipped, first_pair)
        previous = lax.dynamic_index_in_dim(exchange, owner_slot, 0, keepdims=False)
        exchange = lax.dynamic_update_index_in_dim(exchange, previous - pair_term, owner_slot, 0)
        return (exchange, energy + energy_part)

    start_state = (jnp.zeros((own_count, box_edge, plane), jnp.float32), jnp.zeros((), jnp.float32))
    exchange, energy = lax.fori_loop(0, block_count, block_work, start_state)
    exchange_total, replica_energy = lax.psum((exchange, energy), "rep")
    energy_all = lax.psum(replica_energy, ("slab", "orb"))
    orbital_total = own_count * slab_count * orb_count
    exchange_energy = -energy_all / (2.0 * orbital_total * box_edge**3)
    return (exchange_total, exchange_energy.reshape(1))


def solution(mesh):
    in_specs = (
        P(("grp", "slab", "orb"), None, None),
        P("grp", None),
        P(("grp", "slab", "orb"), None),
        P(),
    )
    out_specs = (P(("grp", "slab", "orb"), None, None), P("grp"))
    return jax.shard_map(body, mesh=mesh, in_specs=in_specs, out_specs=out_specs, check_vma=False)
```

profile of v0, /device:TPU:0, one launch (start us, length us, event | category | flops | bytes accessed | tf_op | source)
XLA Modules:
  0.0 167.7 jit_solution(17566683294554462132)
XLA Ops:
  7.2 6.1 %all_gather.3 = bf16[2,32,1024]{2,1,0:T(8,128)(2,1)S(1)} all-gather(bf16[1,32,1024]{2,1,0:T(8,128)(2,1)} %param.9), channel_id=1, replica_groups=mesh['grp'=2,'slab'=4,'orb'=2,'rep'=2] {'orb'}, dimensions={0}, use_global_device_ids=true | all-gather | bytes 196608 | tf_op jit(solution)/shard_map/all_gather | solution.py:95
  13.3 2.1 %collective-permute-start = (bf16[2,32,1024]{2,1,0:T(8,128)(2,1)S(1)}, bf16[2,32,1024]{2,1,0:T(8,128)(2,1)S(1)}, u32[]{:S(2)}, u32[]{:S(2)}) collective-permute-start(bf16[2,32,1024]{2,1,0:T(8,128)(2,1)S(1)} %all_gather.3), channel_id=1, source_target_pairs={{0,4},{4,8},{8,12},{12,0},{1,5},{5,9},{9,13},{13,1},{2,6},{6,10},{... | collective-permute-start | bytes 393224 | tf_op jit(solution)/shard_map/ppermute | solution.py:15
  15.4 2.0 %collective-permute-start.3 = (bf16[2,32,1024]{2,1,0:T(8,128)(2,1)S(1)}, bf16[2,32,1024]{2,1,0:T(8,128)(2,1)S(1)}, u32[]{:S(2)}, u32[]{:S(2)}) collective-permute-start(bf16[2,32,1024]{2,1,0:T(8,128)(2,1)S(1)} %all_gather.3), channel_id=1, source_target_pairs={{0,12},{4,0},{8,4},{12,8},{1,13},{5,1},{9,5},{13,9},{2,14},{6,2},{... | collective-permute-start | bytes 393224 | tf_op jit(solution)/shard_map/ppermute | solution.py:15
  17.4 0.8 copy.13
  18.7 1.3 reduce.13
  21.7 0.8 fusion.67
  22.6 3.9 %collective-permute-start.4 = (bf16[2,32,1024]{2,1,0:T(8,128)(2,1)S(1)}, bf16[2,32,1024]{2,1,0:T(8,128)(2,1)S(1)}, u32[]{:S(2)}, u32[]{:S(2)}) collective-permute-start(bf16[2,32,1024]{2,1,0:T(8,128)(2,1)S(1)} %collective-permute-done.3), channel_id=1, source_target_pairs={{0,12},{4,0},{8,4},{12,8},{1,13},{5,1},{9,5},{13,9},{2,14},{6,2},{... | collective-permute-start | bytes 393224 | tf_op jit(solution)/shard_map/ppermute | solution.py:15
  26.4 2.5 %collective-permute-done.1 = bf16[2,32,1024]{2,1,0:T(8,128)(2,1)S(1)} collective-permute-done((bf16[2,32,1024]{2,1,0:T(8,128)(2,1)S(1)}, bf16[2,32,1024]{2,1,0:T(8,128)(2,1)S(1)}, u32[]{:S(2)}, u32[]{:S(2)}) %collective-permute-start.1) | collective-permute-done | bytes 131104 | tf_op jit(solution)/shard_map/ppermute | solution.py:15
  29.2 4.9 %collective-permute-start.5 = (bf16[2,32,1024]{2,1,0:T(8,128)(2,1)S(1)}, bf16[2,32,1024]{2,1,0:T(8,128)(2,1)S(1)}, u32[]{:S(2)}, u32[]{:S(2)}) collective-permute-start(bf16[2,32,1024]{2,1,0:T(8,128)(2,1)S(1)} %collective-permute-done.4), channel_id=1, source_target_pairs={{0,12},{4,0},{8,4},{12,8},{1,13},{5,1},{9,5},{13,9},{2,14},{6,2},{... | collective-permute-start | bytes 393224 | tf_op jit(solution)/shard_map/ppermute | solution.py:15
  34.1 2.7 %collective-permute-done.2 = bf16[2,32,1024]{2,1,0:T(8,128)(2,1)S(1)} collective-permute-done((bf16[2,32,1024]{2,1,0:T(8,128)(2,1)S(1)}, bf16[2,32,1024]{2,1,0:T(8,128)(2,1)S(1)}, u32[]{:S(2)}, u32[]{:S(2)}) %collective-permute-start.2) | collective-permute-done | bytes 131104 | tf_op jit(solution)/shard_map/ppermute | solution.py:15
  37.3 93.5 %while.20 = (s32[]{:T(128)}, f32[1,32,1024]{2,1,0:T(8,128)S(1)}, f32[]{:T(128)}, f32[12]{0:T(128)S(1)}, bf16[1,32,1024]{2,1,0:T(8,128)(2,1)}, /*index=5*/s32[12,...) while((s32[]{:T(128)}, f32[1,32,1024]{2,1,0:T(8,128)S(1)}, ...), condition=%wide.region_6.7_spmd.clone.clone.clone, body=%wide.region_0.6_spmd.clone.clone.clone.sunk | while | flops 7178883072 | bytes 56513292 | solution.py:153
  37.4 0.8 fusion.96
  38.8 3.7 %fusion.97 = f32[1024,1024]{1,0:T(8,128)} fusion(s32[1024]{0:T(1024)S(1)} %get-tuple-element.785, s32[1024]{0:T(1024)S(1)} %get-tuple-element.784), kind=kLoop, calls=%fused_computation.81.clone.1 | loop fusion | flops 16777216 | bytes 4202496 | tf_op jit(solution)/shard_map/mul | solution.py:59
  42.5 77.8 %conditional.5 = (f32[32,1024]{1,0:T(8,128)S(1)}, f32[]{:T(128)}) conditional(s32[]{:T(128)} %convert_element_type.98, () %tuple.97, (bf16[1,32,1024]{2,1,0:T(8,128)(2,1)S(1)}, s32[12,3]{0,1:T(4,128)S(1)}, s32[]{:T(128)}, s32[12]{0:T(128)S(1)}, bf16[14,32,1024]{2,1,0:T(8,128)(2,1)S(1)}, /*index=5*/f32[4]{0:T(128)S(1)}, f32[1024,1024]{1,0:T(8,128)}, ...), branch_computations={%region_2.2_spmd, %region_3.5_spmd.clone} | conditional | flops 7162058752 | bytes 51126648 | solution.py:147
  43.3 4.2 %fusion.38 = f32[4,32,1024]{2,1,0:T(8,128)S(1)} fusion(s32[4]{0:T(128)S(1)} %get-tuple-element.652, s32[1024]{0:T(1024)S(1)} %get-tuple-element.655, s32[1024]{0:T(1024)S(1)} %get-tuple-element.656, s32[4]{0:T(128)S(1)} %get-tuple-element.653, s32[1024]{0:T(1024)S(1)} %get-tuple-element.654, s32[1024]{0:T(1024)S(1)} %get-tuple-element.657, ...), kind=kOutput, calls=%fused_computation.44 | convolution fusion | flops 314843136 | bytes 804928 | tf_op jit(solution)/shard_map/while/body/eval_jaxpr/cond/branch_1_fun/pam,pmn->pan/dot_general | solution.py:44
  47.5 17.6 %fusion.31 = f32[4,32,1024]{2,1,0:T(8,128)S(1)} fusion(f32[1024,1024]{1,0:T(8,128)} %get-tuple-element.609, f32[4,32,1024]{2,1,0:T(8,128)S(1)} %fusion.38, f32[32,1024]{1,0:T(8,128)S(1)} %bitcast_convert_fusion), kind=kOutput, calls=%fused_computation.33 | convolution fusion | flops 1610874880 | bytes 5373952 | tf_op jit(solution)/shard_map/while/body/eval_jaxpr/cond/branch_1_fun/pam,mn->pan/dot_general | solution.py:68
  65.1 16.2 %fusion.26 = f32[4,32,1024]{2,1,0:T(8,128)S(1)} fusion(f32[1024,1024]{1,0:T(8,128)S(1)} %copy-done, f32[4,32,1024]{2,1,0:T(8,128)S(1)} %fusion.38, f32[32,1024]{1,0:T(8,128)S(1)} %bitcast_convert_fusion), kind=kOutput, calls=%fused_computation.28 | convolution fusion | flops 1610743808 | bytes 5373952 | tf_op jit(solution)/shard_map/while/body/eval_jaxpr/cond/branch_1_fun/pam,mn->pan/dot_general | solution.py:68
  86.7 16.2 %fusion.25 = f32[4,32,1024]{2,1,0:T(8,128)S(1)} fusion(f32[4,32,1024]{2,1,0:T(8,128)S(1)} %fusion.33, f32[1024,1024]{1,0:T(8,128)S(1)} %copy-done), kind=kOutput, calls=%fused_computation.27 | convolution fusion | flops 1610612736 | bytes 5242880 | tf_op jit(solution)/shard_map/while/body/eval_jaxpr/cond/branch_1_fun/pam,mn->pan/dot_general | solution.py:68
  102.9 16.7 %multiply_reduce_fusion = (f32[]{:T(128)}, f32[32,1024]{1,0:T(8,128)S(1)}) fusion(f32[4,32,1024]{2,1,0:T(8,128)S(1)} %fusion.38, f32[32,1024]{1,0:T(8,128)S(1)} %bitcast_convert_fusion, f32[4,32,1024]{2,1,0:T(8,128)S(1)} %fusion.25, f32[4,32,1024]{2,1,0:T(8,128)S(1)} %fusion.32, f32[1024,1024]{1,0:T(8,128)S(1)} %copy-done), kind=kOutput, calls=%fused_computation.46 | convolution fusion | flops 1611497472 | bytes 6029316 | tf_op jit(solution)/shard_map/while/body/eval_jaxpr/cond/branch_1_fun/pam,mn->pan/dot_general | solution.py:68
  121.8 3.7 %fusion.97 = f32[1024,1024]{1,0:T(8,128)} fusion(s32[1024]{0:T(1024)S(1)} %get-tuple-element.785, s32[1024]{0:T(1024)S(1)} %get-tuple-element.784), kind=kLoop, calls=%fused_computation.81.clone.1 | loop fusion | flops 16777216 | bytes 4202496 | tf_op jit(solution)/shard_map/mul | solution.py:59
  127.1 3.7 %fusion.97 = f32[1024,1024]{1,0:T(8,128)} fusion(s32[1024]{0:T(1024)S(1)} %get-tuple-element.785, s32[1024]{0:T(1024)S(1)} %get-tuple-element.784), kind=kLoop, calls=%fused_computation.81.clone.1 | loop fusion | flops 16777216 | bytes 4202496 | tf_op jit(solution)/shard_map/mul | solution.py:59
  131.5 3.7 %psum.22 = f32[]{:T(128)} all-reduce(f32[]{:T(128)} %get-tuple-element.447), channel_id=1, replica_groups=mesh['grp'=2,'slab'=4,'orb'=2,'rep'=2] {'rep'}, use_global_device_ids=true, to_apply=%region_8.9 | all-reduce | flops 1 | bytes 8 | tf_op jit(solution)/shard_map/psum | solution.py:154
  135.2 22.3 %psum.23 = f32[]{:T(128)} all-reduce(f32[]{:T(128)} %psum.22), channel_id=1, replica_groups=mesh['grp'=2,'slab'=4,'orb'=2,'rep'=2] {'slab','orb'}, use_global_device_ids=true, to_apply=%region_9.10 | all-reduce | flops 1 | bytes 8 | tf_op jit(solution)/shard_map/psum | solution.py:155
  158.2 1.6 copy.38
  (74 shorter events, 11.5 us)
Async XLA Ops:
  7.2 151.0 %all-reduce.2.cloned.1.call-start = ((), (), s32[]{:S(2)}) async-start(), calls=%async_computation | async-start | bytes 262144 | tf_op jit(solution)/shard_map/psum | solution.py:154
  13.3 8.3 %collective-permute-start = (bf16[2,32,1024]{2,1,0:T(8,128)(2,1)S(1)}, bf16[2,32,1024]{2,1,0:T(8,128)(2,1)S(1)}, u32[]{:S(2)}, u32[]{:S(2)}) collective-permute-start(bf16[2,32,1024]{2,1,0:T(8,128)(2,1)S(1)} %all_gather.3), channel_id=1, source_target_pairs={{0,4},{4,8},{8,12},{12,0},{1,5},{5,9},{9,13},{13,1},{2,6},{6,10},{... | collective-permute-start | bytes 393224 | tf_op jit(solution)/shard_map/ppermute | solution.py:15
  15.4 7.2 %collective-permute-start.3 = (bf16[2,32,1024]{2,1,0:T(8,128)(2,1)S(1)}, bf16[2,32,1024]{2,1,0:T(8,128)(2,1)S(1)}, u32[]{:S(2)}, u32[]{:S(2)}) collective-permute-start(bf16[2,32,1024]{2,1,0:T(8,128)(2,1)S(1)} %all_gather.3), channel_id=1, source_target_pairs={{0,12},{4,0},{8,4},{12,8},{1,13},{5,1},{9,5},{13,9},{2,14},{6,2},{... | collective-permute-start | bytes 393224 | tf_op jit(solution)/shard_map/ppermute | solution.py:15
  21.7 7.2 %collective-permute-start.1 = (bf16[2,32,1024]{2,1,0:T(8,128)(2,1)S(1)}, bf16[2,32,1024]{2,1,0:T(8,128)(2,1)S(1)}, u32[]{:S(2)}, u32[]{:S(2)}) collective-permute-start(bf16[2,32,1024]{2,1,0:T(8,128)(2,1)S(1)} %collective-permute-done), channel_id=1, source_target_pairs={{0,4},{4,8},{8,12},{12,0},{1,5},{5,9},{9,13},{13,1},{2,6},{6,10},{... | collective-permute-start | bytes 393224 | tf_op jit(solution)/shard_map/ppermute | solution.py:15
  22.6 6.7 %collective-permute-start.4 = (bf16[2,32,1024]{2,1,0:T(8,128)(2,1)S(1)}, bf16[2,32,1024]{2,1,0:T(8,128)(2,1)S(1)}, u32[]{:S(2)}, u32[]{:S(2)}) collective-permute-start(bf16[2,32,1024]{2,1,0:T(8,128)(2,1)S(1)} %collective-permute-done.3), channel_id=1, source_target_pairs={{0,12},{4,0},{8,4},{12,8},{1,13},{5,1},{9,5},{13,9},{2,14},{6,2},{... | collective-permute-start | bytes 393224 | tf_op jit(solution)/shard_map/ppermute | solution.py:15
  28.9 7.9 %collective-permute-start.2 = (bf16[2,32,1024]{2,1,0:T(8,128)(2,1)S(1)}, bf16[2,32,1024]{2,1,0:T(8,128)(2,1)S(1)}, u32[]{:S(2)}, u32[]{:S(2)}) collective-permute-start(bf16[2,32,1024]{2,1,0:T(8,128)(2,1)S(1)} %collective-permute-done.1), channel_id=1, source_target_pairs={{0,4},{4,8},{8,12},{12,0},{1,5},{5,9},{9,13},{13,1},{2,6},{6,10},{... | collective-permute-start | bytes 393224 | tf_op jit(solution)/shard_map/ppermute | solution.py:15
  29.2 8.0 %collective-permute-start.5 = (bf16[2,32,1024]{2,1,0:T(8,128)(2,1)S(1)}, bf16[2,32,1024]{2,1,0:T(8,128)(2,1)S(1)}, u32[]{:S(2)}, u32[]{:S(2)}) collective-permute-start(bf16[2,32,1024]{2,1,0:T(8,128)(2,1)S(1)} %collective-permute-done.4), channel_id=1, source_target_pairs={{0,12},{4,0},{8,4},{12,8},{1,13},{5,1},{9,5},{13,9},{2,14},{6,2},{... | collective-permute-start | bytes 393224 | tf_op jit(solution)/shard_map/ppermute | solution.py:15
  37.3 5.2 %copy-start.1 = (f32[32,1024]{1,0:T(8,128)S(1)}, f32[32,1024]{1,0:T(8,128)}, u32[]{:S(2)}) copy-start(f32[32,1024]{1,0:T(8,128)} %get-tuple-element.783) | copy-start | bytes 393220 | tf_op jit(solution)/shard_map/while
  37.3 5.2 %copy-start.3 = (bf16[1,32,1024]{2,1,0:T(8,128)(2,1)S(1)}, bf16[1,32,1024]{2,1,0:T(8,128)(2,1)}, u32[]{:S(2)}) copy-start(bf16[1,32,1024]{2,1,0:T(8,128)(2,1)} %get-tuple-element.779) | copy-start | bytes 196612 | tf_op jit(solution)/shard_map/while
  47.5 17.6 %copy-start = (f32[1024,1024]{1,0:T(8,128)S(1)}, f32[1024,1024]{1,0:T(8,128)}, u32[]{:S(2)}) copy-start(f32[1024,1024]{1,0:T(8,128)} %get-tuple-element.609) | copy-start | bytes 12582916 | tf_op jit(solution)/shard_map/while/body/eval_jaxpr/cond
  120.3 5.2 %copy-start.1 = (f32[32,1024]{1,0:T(8,128)S(1)}, f32[32,1024]{1,0:T(8,128)}, u32[]{:S(2)}) copy-start(f32[32,1024]{1,0:T(8,128)} %get-tuple-element.783) | copy-start | bytes 393220 | tf_op jit(solution)/shard_map/while
  120.3 5.2 %copy-start.3 = (bf16[1,32,1024]{2,1,0:T(8,128)(2,1)S(1)}, bf16[1,32,1024]{2,1,0:T(8,128)(2,1)}, u32[]{:S(2)}) copy-start(bf16[1,32,1024]{2,1,0:T(8,128)(2,1)} %get-tuple-element.779) | copy-start | bytes 196612 | tf_op jit(solution)/shard_map/while
  125.6 5.2 %copy-start.1 = (f32[32,1024]{1,0:T(8,128)S(1)}, f32[32,1024]{1,0:T(8,128)}, u32[]{:S(2)}) copy-start(f32[32,1024]{1,0:T(8,128)} %get-tuple-element.783) | copy-start | bytes 393220 | tf_op jit(solution)/shard_map/while
  125.6 5.2 %copy-start.3 = (bf16[1,32,1024]{2,1,0:T(8,128)(2,1)S(1)}, bf16[1,32,1024]{2,1,0:T(8,128)(2,1)}, u32[]{:S(2)}) copy-start(bf16[1,32,1024]{2,1,0:T(8,128)(2,1)} %get-tuple-element.779) | copy-start | bytes 196612 | tf_op jit(solution)/shard_map/while
  130.9 0.7 copy-start.2
Sparse Core Ops, SparseCore 0:
  131.7 19.1 all-reduce.1
where the time goes:
time: 168 us
  matrix products  76.2 us (45%)
  blocking collectives  32.1 us (19%)
  other arithmetic  16.2 us (10%)
  between operations  15.9 us (9%)
  starting transfers between devices  12.9 us (8%)
  local copies, waits for them, and re-layouts  5.64 us (3%)
  waiting for transfers between devices  5.57 us (3%)
  loops' own time  3.13 us (2%)
    dot_general x4, matrix products, plane_turn(): jnp.einsum('pam,mn->pan', values, table, precision=lax.Precision.HIGHEST)  66.7 us
    psum x1, blocking collectives, body(): energy_all = lax.psum(replica_energy, ('slab', 'orb'))  22.3 us
    ppermute x6, starting transfers between devices, passed_along(): lax.ppermute(array, axis, [(i, (i + by) % size) for i in range(size)])  12.9 us
    mul x3, other arithmetic, fourier_tables(): plane_angles = plane_phases.astype(jnp.float32) * (2.0 * math.pi / box_edge)  11 us
    all_gather x1, blocking collectives, body(): gathered = lax.all_gather(orbitals, 'orb', axis=0, tiled=True)  6.14 us
    ppermute x6, waiting for transfers between devices, passed_along(): lax.ppermute(array, axis, [(i, (i + by) % size) for i in range(size)])  5.54 us
    dot_general x8, matrix products, edge_rotation(): jnp.einsum('ka,pam->pkm', matrix, values, precision=lax.Precision.HIGHEST)  5.3 us
    dot_general x1, matrix products, place_boxes(): jnp.einsum('pam,pmn->pan', displaced_density, step_plane, preferred_eleme...  4.2 us
  transfers between devices with their start and end apart: 7, of which 4 were waited for; matrix products, arithmetic and copies ran while one was open for 3% of the time, Pallas kernels for 0%

commit v1 on v0

v1 whole, which is shorter than its diff:
```python
import functools
import math

import jax
import jax.numpy as jnp
import numpy as np
from jax import lax
from jax.experimental import pallas as pl
from jax.experimental.pallas import tpu as pltpu
from jax.sharding import PartitionSpec as P

G = 192
ZDEV = 12
RADIX = 4
FIELDS = 2
MESH = pl.DeviceIdType.MESH


def split_np(values):
    high = values.astype(jnp.bfloat16)
    low = (values - high.astype(np.float64)).astype(jnp.bfloat16)
    return high, low


@functools.lru_cache(None)
def tables(edge):
    inner = edge // RADIX
    part = inner * edge
    turn = 2.0 * math.pi / edge
    ids = np.arange(edge)
    angles = (ids[:, None] * ids[None, :] % edge) * turn
    cosine, sine = np.cos(angles), np.sin(angles)
    edge_table = np.block([[cosine, sine], [-sine, cosine]])
    high, low = split_np(edge_table)
    edge_stack = np.concatenate([high, high, low], axis=1)
    lanes = np.arange(part)
    lane_b, lane_c = lanes // edge, lanes % edge
    phases = (RADIX * lane_b[:, None] * lane_b[None, :] + lane_c[:, None] * lane_c[None, :]) % edge
    cosine, sine = np.cos(phases * turn), np.sin(phases * turn)
    blocks = []
    for half in (np.concatenate([cosine, -sine], axis=1), np.concatenate([sine, cosine], axis=1)):
        high, low = split_np(half)
        blocks += [high, high, low]
    plane_stack = np.concatenate(blocks, axis=0)
    twiddle = []
    for first in range(RADIX):
        phase = (lane_b * first % edge) * turn
        twiddle += [np.cos(phase), np.sin(phase)]
    twiddle = np.stack(twiddle).astype(np.float32)
    flips = []
    for outer in (-lane_b % inner, inner - 1 - lane_b):
        source = outer * edge + (-lane_c % edge)
        flips.append((lanes[:, None] == source[None, :]).astype(jnp.bfloat16))
    flips = np.stack(flips)
    rows = (ids[:, None] == (-ids % edge)[None, :]).astype(jnp.bfloat16)
    row_flip = np.concatenate([rows, rows], axis=1)
    return edge_stack, plane_stack, twiddle, flips, row_flip


def parts(values):
    high = values.astype(jnp.bfloat16)
    return high, (values - high.astype(jnp.float32)).astype(jnp.bfloat16)


def dot(left, right):
    return jnp.dot(left, right, preferred_element_type=jnp.float32)


def butterfly(re, im):
    sum_re, sum_im = re[0] + re[2], im[0] + im[2]
    dif_re, dif_im = re[0] - re[2], im[0] - im[2]
    odd_re, odd_im = re[1] + re[3], im[1] + im[3]
    gap_re, gap_im = re[1] - re[3], im[1] - im[3]
    return (
        [sum_re + odd_re, dif_re + gap_im, sum_re - odd_re, dif_re - gap_im],
        [sum_im + odd_im, dif_im - gap_re, sum_im - odd_im, dif_im + gap_re],
    )


def twiddled(re, im, first, twiddle):
    if first == 0:
        return re, im
    cosine, sine = twiddle[2 * first : 2 * first + 1], twiddle[2 * first + 1 : 2 * first + 2]
    return re * cosine + im * sine, im * cosine - re * sine


def plane_turn(blocks, plane_table):
    rows = []
    for re, im in blocks:
        re_high, re_low = parts(re)
        im_high, im_low = parts(im)
        rows.append(
            jnp.concatenate([re_high, re_low, re_high, im_high, im_low, im_high], axis=1)
        )
    result = dot(jnp.concatenate(rows, axis=0), plane_table)
    edge, part = blocks[0][0].shape
    return [
        (result[n * edge : (n + 1) * edge, :part], result[n * edge : (n + 1) * edge, part:])
        for n in range(len(blocks))
    ]


def edge_turn(block, edge_table):
    re, im = block
    edge = re.shape[0]
    re_high, re_low = parts(re)
    im_high, im_low = parts(im)
    column = jnp.concatenate([re_high, im_high, re_low, im_low, re_high, im_high], axis=0)
    result = dot(edge_table, column)
    return result[:edge], result[edge:]


def prepared_kernel(values, flips, row_flip, edge):
    inner = edge // RADIX
    part = inner * edge
    width = RADIX * edge
    segment = lax.broadcasted_iota(jnp.int32, (edge, width), 1) // edge
    chunks = []
    for first in range(RADIX):
        pieces = []
        for group in range(part // width):
            piece = None
            for place in range(RADIX):
                source = RADIX * group + place
                moved = values[:, source * width : (source + 1) * width]
                shift = (place - first) * edge % width
                if shift:
                    moved = pltpu.roll(moved, shift, 1)
                piece = moved if piece is None else jnp.where(segment == place, moved, piece)
            pieces.append(piece)
        chunks.append(jnp.concatenate(pieces, axis=1))
    scale = 0.5 / float(edge**3)
    result = []
    for first in range(RADIX):
        high, low = parts(chunks[-first % RADIX])
        flip = flips[0] if first == 0 else flips[1]
        swapped = dot(jnp.concatenate([high, low], axis=0), flip).astype(jnp.bfloat16)
        result.append((chunks[first] + dot(row_flip, swapped)) * scale)
    return result


def fused(
    cfg,
    partners,
    corners,
    orbital,
    kernel,
    edge_table,
    plane_hbm,
    twiddle_ref,
    flips,
    row_flip,
    mine,
    theirs,
    energy_out,
    boxes,
    plane_table,
    spectrum,
    energies,
    table_sem,
    box_send,
    box_recv,
    fwd_send,
    fwd_recv,
    out_send,
    out_recv,
    energy_send,
    energy_recv,
):
    slabs, orbs, reps, steps, shift_back, slot_count, stages = cfg
    edge, plane = orbital.shape[1], orbital.shape[2]
    slab, orb, rep = lax.axis_index("slab"), lax.axis_index("orb"), lax.axis_index("rep")
    sizes = {"slab": slabs, "orb": orbs, "rep": reps}
    here = {"slab": slab, "orb": orb, "rep": rep}

    def place(moves):
        return {a: lax.rem(here[a] + moves[a] % sizes[a], sizes[a]) for a in moves}

    box_moves = [(t, u) for t in steps for u in range(orbs) if (t % slabs, u) != (0, 0)]
    reached = {(t % slabs, u, 0) for t, u in box_moves} | {(0, 0, v) for v in range(1, reps)}
    stage_moves = []
    for axes in stages:
        moves = [{}]
        for a in axes:
            moves = [dict(m, **{a: n}) for m in moves for n in range(sizes[a])]
        stage_moves.append([m for m in moves if any(m.values())])
        reached |= {(m.get("slab", 0), m.get("orb", 0), m.get("rep", 0)) for m in stage_moves[-1]}
    reached |= {(-t % slabs, -u % orbs, -v % reps) for t, u, v in reached}
    reached = sorted(reached)

    table_copy = pltpu.make_async_copy(plane_hbm, plane_table, table_sem)
    table_copy.start()
    barrier = pltpu.get_barrier_semaphore()
    for t, u, v in reached:
        pl.semaphore_signal(
            barrier,
            inc=1,
            device_id=place({"slab": t, "orb": u, "rep": v}),
            device_id_type=MESH,
        )
    pl.semaphore_wait(barrier, len(reached))

    def slot_of(t, u):
        return (t + shift_back) % slabs * orbs + u % orbs

    cut = edge // reps
    share = pl.ds(pl.multiple_of(rep * cut, cut), cut)
    sends = []
    for t, u in box_moves:
        target = slot_of(-t, -u)
        copy = pltpu.make_async_remote_copy(
            src_ref=orbital.at[0, share],
            dst_ref=boxes.at[target, share],
            send_sem=box_send.at[target],
            recv_sem=box_recv.at[target],
            device_id=place({"slab": t, "orb": u}),
            device_id_type=MESH,
        )
        copy.start()
        sends.append((slot_of(t, u), copy))

    centre = orbital[0].astype(jnp.float32)
    boxes[slot_of(0, 0)] = orbital[0]
    for n, chunk in enumerate(prepared_kernel(kernel[...], flips, row_flip[...], edge)):
        spectrum[n] = chunk
    twiddle = twiddle_ref[...]
    edge_tab = edge_table[...]

    forwards = []
    for t, u in box_moves:
        slot = slot_of(t, u)
        pltpu.make_async_remote_copy(
            src_ref=orbital.at[0, share],
            dst_ref=boxes.at[slot, share],
            send_sem=box_send.at[slot],
            recv_sem=box_recv.at[slot],
            device_id=place({"slab": t, "orb": u}),
            device_id_type=MESH,
        ).wait_recv()
        for v in range(1, reps):
            copy = pltpu.make_async_remote_copy(
                src_ref=boxes.at[slot, share],
                dst_ref=boxes.at[slot, share],
                send_sem=fwd_send.at[slot, v],
                recv_sem=fwd_recv.at[slot, v],
                device_id=place({"rep": v}),
                device_id_type=MESH,
            )
            copy.start()
            forwards.append(copy)
    table_copy.wait()
    for copy in forwards:
        copy.wait()

    lengths = (G, G, ZDEV * slabs)
    lane = lax.broadcasted_iota(jnp.int32, (1, plane), 1)
    lane_b, lane_c = lane // edge, lane % edge
    row = lax.broadcasted_iota(jnp.int32, (edge, 1), 0)
    own_row = slab * orbs + orb

    def moved_box(number):
        partner = partners[0, number * reps + rep]
        known = jnp.maximum(partner, 0)
        offsets = []
        for axis, length in enumerate(lengths):
            delta = corners[own_row, axis] - corners[known, axis]
            delta = jnp.where(delta < -(length // 2), delta + length, delta)
            delta = jnp.where(delta >= length - length // 2, delta - length, delta)
            offsets.append(delta)
        along_a, along_b, along_c = offsets
        step = known // orbs - slab + shift_back + 2 * slabs
        turn = lax.rem(known % orbs - orb + orbs, orbs)
        slot = jnp.minimum(lax.rem(step, slabs) * orbs + turn, boxes.shape[0] - 1)
        box = boxes[slot].astype(jnp.float32)
        box = pltpu.roll(box, (2 * plane - along_b * edge - along_c) % plane, 1)
        box = pltpu.roll(box, (2 * edge - along_a) % edge, 0)
        from_a, from_b, from_c = row + along_a, lane_b + along_b, lane_c + along_c
        usable = jnp.where(partner >= 0, edge, 0)
        inside_a = (from_a >= 0) & (from_a < usable)
        inside = (from_b >= 0) & (from_b < edge) & (from_c >= 0) & (from_c < edge)
        return jnp.where(inside_a & inside, box, 0.0)

    part = plane // RADIX
    cuts = [slice(n * part, (n + 1) * part) for n in range(RADIX)]
    total = jnp.zeros((edge, plane), jnp.float32)
    for start in range(0, slot_count, 2 * FIELDS):
        moved = [moved_box(n) for n in range(start, min(start + 2 * FIELDS, slot_count))]
        if len(moved) % 2:
            moved.append(jnp.zeros((edge, plane), jnp.float32))
        blocks = []
        for n in range(0, len(moved), 2):
            re, im = centre * moved[n], centre * moved[n + 1]
            re, im = butterfly([re[:, c] for c in cuts], [im[:, c] for c in cuts])
            blocks += [twiddled(re[k], im[k], k, twiddle) for k in range(RADIX)]
        blocks = plane_turn(blocks, plane_table[...])
        for n, block in enumerate(blocks):
            re, im = edge_turn(block, edge_tab)
            factor = spectrum[n % RADIX]
            blocks[n] = edge_turn((re * factor, -im * factor), edge_tab)
        blocks = plane_turn(blocks, plane_table[...])
        for n in range(0, len(moved), 2):
            field = blocks[n // 2 * RADIX : (n // 2 + 1) * RADIX]
            field = [twiddled(re, im, k, twiddle) for k, (re, im) in enumerate(field)]
            re, im = butterfly([f[0] for f in field], [f[1] for f in field])
            re, im = jnp.concatenate(re, axis=1), jnp.concatenate(im, axis=1)
            total = total + (im * moved[n + 1] - re * moved[n])
    mine[0] = total
    weighed = centre * total
    tile = weighed[:, :128]
    for n in range(128, plane, 128):
        tile = tile + weighed[:, n : n + 128]
    tile = sum(tile[n : n + 8] for n in range(8, edge, 8)) + tile[:8]

    swaps = []
    for v in range(1, reps):
        copy = pltpu.make_async_remote_copy(
            src_ref=mine,
            dst_ref=theirs.at[pl.ds(v - 1, 1)],
            send_sem=out_send.at[v - 1],
            recv_sem=out_recv.at[v - 1],
            device_id=place({"rep": v}),
            device_id_type=MESH,
        )
        copy.start()
        swaps.append(copy)

    for stage, (axes, moves) in enumerate(zip(stages, stage_moves)):
        count = math.prod(sizes[a] for a in axes)

        def number(moved):
            result = 0
            for a in axes:
                result = result * sizes[a] + moved.get(a, here[a])
            return result

        me = number({})
        energies[stage, me] = tile
        copies = []
        for n, m in enumerate(moves):
            copies.append(
                pltpu.make_async_remote_copy(
                    src_ref=energies.at[stage, me],
                    dst_ref=energies.at[stage, me],
                    send_sem=energy_send.at[stage, n],
                    recv_sem=energy_recv.at[stage, n],
                    device_id=place(m),
                    device_id_type=MESH,
                )
            )
            copies[-1].start()
        for copy in copies:
            copy.wait()
        tile = energies[stage, 0]
        for n in range(1, count):
            tile = tile + energies[stage, n]
    orbital_total = slabs * orbs
    value = jnp.sum(tile, keepdims=True) * (1.0 / (2.0 * orbital_total * edge**3))
    energy_out[...] = jnp.broadcast_to(value, energy_out.shape)
    for copy in swaps:
        copy.wait()
    for _, copy in sends:
        copy.wait_send()


def body(orbitals, corners, partners, kernel):
    own_count, edge, plane = orbitals.shape
    assert own_count == 1
    slabs, orbs, reps = (lax.axis_size(a) for a in ("slab", "orb", "rep"))
    depth = (ZDEV + edge - 2) // ZDEV
    if slabs <= 2 * depth + 1:
        steps, shift_back = tuple(range(slabs)), 0
    else:
        steps, shift_back = tuple(range(-depth, depth + 1)), depth
    slot_count = -(-min(partners.shape[1], slabs * orbs) // reps)
    if slabs * orbs * reps <= 16:
        stages = (("slab", "orb", "rep"),)
    else:
        stages = (("orb", "rep"), ("slab",))
    sizes = {"slab": slabs, "orb": orbs, "rep": reps}
    widest = max(math.prod(sizes[a] for a in axes) for axes in stages)
    cfg = (slabs, orbs, reps, steps, shift_back, slot_count, stages)
    edge_stack, plane_stack, twiddle, flips, row_flip = tables(edge)
    count = len(steps) * orbs
    vmem = pl.BlockSpec(memory_space=pltpu.VMEM)
    smem = pl.BlockSpec(memory_space=pltpu.SMEM)
    dma = pltpu.SemaphoreType.DMA
    mine, theirs, energy = pl.pallas_call(
        functools.partial(fused, cfg),
        out_shape=(
            jax.ShapeDtypeStruct((1, edge, plane), jnp.float32),
            jax.ShapeDtypeStruct((max(reps - 1, 1), edge, plane), jnp.float32),
            jax.ShapeDtypeStruct((8, 128), jnp.float32),
        ),
        in_specs=[smem, smem, vmem, vmem, vmem, pl.BlockSpec(memory_space=pl.ANY), vmem, vmem, vmem],
        out_specs=(vmem, vmem, vmem),
        scratch_shapes=[
            pltpu.VMEM((count, edge, plane), jnp.bfloat16),
            pltpu.VMEM(plane_stack.shape, jnp.bfloat16),
            pltpu.VMEM((RADIX, edge, plane // RADIX), jnp.float32),
            pltpu.VMEM((len(stages), widest, 8, 128), jnp.float32),
            dma,
            dma((count,)),
            dma((count,)),
            dma((count, reps)),
            dma((count, reps)),
            dma((reps,)),
            dma((reps,)),
            dma((len(stages), widest)),
            dma((len(stages), widest)),
        ],
        compiler_params=pltpu.CompilerParams(collective_id=0, has_side_effects=True),
    )(
        partners,
        corners,
        orbitals,
        kernel,
        jnp.asarray(edge_stack),
        jnp.asarray(plane_stack),
        jnp.asarray(twiddle),
        jnp.asarray(flips),
        jnp.asarray(row_flip),
    )
    result = mine
    for v in range(reps - 1):
        result = result + theirs[v : v + 1]
    return result, energy[0, :1]


def solution(mesh):
    in_specs = (
        P(("grp", "slab", "orb"), None, None),
        P("grp", None),
        P(("grp", "slab", "orb"), None),
        P(),
    )
    out_specs = (P(("grp", "slab", "orb"), None, None), P("grp"))
    return jax.shard_map(body, mesh=mesh, in_specs=in_specs, out_specs=out_specs, check_vma=False)
```

time: 168 us -> 29 us (0.17)
  matrix products: 76.2 us -> 0 us
  blocking collectives: 32.1 us -> 0 us
  Pallas kernels: 0 us -> 23.9 us
  between operations: 15.9 us -> 0.64 us
  other arithmetic: 16.2 us -> 1.64 us
  starting transfers between devices: 12.9 us -> 0 us
  waiting for transfers between devices: 5.57 us -> 0 us
  loops' own time: 3.13 us -> 0 us
  local copies, waits for them, and re-layouts: 5.64 us -> 2.54 us
    dot_general x13 -> x0, matrix products: 76.2 us -> none  [the longest x4 66.7 us: plane_turn(): jnp.einsum('pam,mn->pan', values, table, precision=lax.Precision.HIGHEST)]
    psum x2 -> x0, blocking collectives: 26 us -> none  [the longest x1 22.3 us: body(): energy_all = lax.psum(replica_energy, ('slab', 'orb'))]
    pallas_call x0 -> x1, Pallas kernels: none -> 23.9 us  [body(): pl.pallas_call(functools.partial(fused, cfg), out_shape=(jax.ShapeDtypeSt...]
    ppermute x6 -> x0, starting transfers between devices: 12.9 us -> none  [passed_along(): lax.ppermute(array, axis, [(i, (i + by) % size) for i in range(size)])]
    mul x7 -> x0, other arithmetic: 11.1 us -> none  [the longest x3 11 us: fourier_tables(): plane_angles = plane_phases.astype(jnp.float32) * (2.0 * math.pi / box_edge)]
    all_gather x1 -> x0, blocking collectives: 6.14 us -> none  [body(): gathered = lax.all_gather(orbitals, 'orb', axis=0, tiled=True)]
    ppermute x6 -> x0, waiting for transfers between devices: 5.54 us -> none  [passed_along(): lax.ppermute(array, axis, [(i, (i + by) % size) for i in range(size)])]
    another operation x4 -> x0, loops' own time: 3.13 us -> none  [the longest x1 2.29 us: body(): exchange, energy = lax.fori_loop(0, block_count, block_work, start_state)]
  transfers between devices with their start and end apart: 7 -> 0, of which waited for: 4 -> 0; matrix products, arithmetic and copies ran while one was open for 3% -> 0% of each run, Pallas kernels for 0% -> 0%
where the time goes in v1:
time: 29 us; the launch traced here: 28.8 us
  Pallas kernels  23.9 us (82%)
  local copies, waits for them, and re-layouts  2.54 us (9%)
  other arithmetic  1.64 us (6%)
  between operations  0.64 us (2%)
    pallas_call x1, Pallas kernels, body(): pl.pallas_call(functools.partial(fused, cfg), out_shape=(jax.ShapeDtypeSt...  23.9 us
    add x1, other arithmetic, body(): result = result + theirs[v:v + 1]  1.64 us
    unnamed x1, local copies, waits for them, and re-layouts  1.35 us
    slice x1, local copies, waits for them, and re-layouts, body(): return (result, energy[0, :1])  1.2 us

profile of v1, /device:TPU:0, one launch (start us, length us, event | category | flops | bytes accessed | tf_op | source)
XLA Modules:
  0.0 28.8 jit_solution(4392731387994031294)
XLA Ops:
  0.6 1.3 %copy.11.corners = s32[8,3]{1,0:T(8,128)} copy(s32[8,3]{0,1:T(4,128)} %param.10) | data formatting | bytes 192 | tf_op args[1]
  2.0 23.9 %shard_map.104 = (f32[1,32,1024]{2,1,0:T(8,128)}, f32[1,32,1024]{2,1,0:T(8,128)}, f32[8,128]{1,0:T(8,128)}) custom-call(s32[1,24]{1,0:T(1,128)} %partners.1, s32[8,3]{1,0:T(8,128)} %copy.11.corners, bf16[1,32,1024]{2,1,0:T(8,128)(2,1)} %orbital.1, f32[32,1024]{1,0:T(8,128)} %kernel.1, bf16[64,192]{1,0:T(8,128)(2,1)} %constant.10.clone.edge_table, ...), custom_call_target="tpu_custom_call" | custom-call | tf_op jit(solution)/shard_map/pallas_call | solution.py:387
  25.9 1.2 %slice.3 = f32[1,1]{1,0:T(1,128)} slice(f32[8,128]{1,0:T(8,128)} %get-tuple-element.7), slice={[0:1], [0:1]} | slice | bytes 8 | tf_op jit(solution)/shard_map/slice | solution.py:426
  27.1 1.6 %add.3 = f32[1,32,1024]{2,1,0:T(8,128)} add(f32[1,32,1024]{2,1,0:T(8,128)} %get-tuple-element.5, f32[1,32,1024]{2,1,0:T(8,128)} %get-tuple-element.6) | non-fusion elementwise | flops 32768 | bytes 393216 | tf_op jit(solution)/shard_map/add | solution.py:425

commit v2 on v1

--- a/solution.py
+++ b/solution.py
@@ -141,32 +141,43 @@
 
 def fused(
     cfg,
-    partners,
-    corners,
-    orbital,
-    kernel,
-    edge_table,
-    plane_hbm,
-    twiddle_ref,
-    flips,
-    row_flip,
-    mine,
-    theirs,
-    energy_out,
-    boxes,
-    plane_table,
-    spectrum,
-    energies,
-    table_sem,
-    box_send,
-    box_recv,
-    fwd_send,
-    fwd_recv,
-    out_send,
-    out_recv,
-    energy_send,
-    energy_recv,
+    *refs,
 ):
+    (
+        partners_hbm,
+        corners_hbm,
+        orbital_hbm,
+        kernel_hbm,
+        edge_hbm,
+        plane_hbm,
+        twiddle_hbm,
+        flips_hbm,
+        row_hbm,
+        mine,
+        theirs,
+        energy_out,
+        partners,
+        corners,
+        orbital,
+        kernel,
+        edge_table,
+        twiddle_ref,
+        flips,
+        row_flip,
+        boxes,
+        plane_table,
+        spectrum,
+        energies,
+        load_sem,
+        box_send,
+        box_recv,
+        fwd_send,
+        fwd_recv,
+        out_send,
+        out_recv,
+        energy_send,
+        energy_recv,
+    ) = refs
     slabs, orbs, reps, steps, shift_back, slot_count, stages = cfg
     edge, plane = orbital.shape[1], orbital.shape[2]
     slab, orb, rep = lax.axis_index("slab"), lax.axis_index("orb"), lax.axis_index("rep")
@@ -188,8 +199,24 @@
     reached |= {(-t % slabs, -u % orbs, -v % reps) for t, u, v in reached}
     reached = sorted(reached)
 
-    table_copy = pltpu.make_async_copy(plane_hbm, plane_table, table_sem)
-    table_copy.start()
+    loads = [
+        pltpu.make_async_copy(source, target, load_sem.at[n])
+        for n, (source, target) in enumerate(
+            [
+                (orbital_hbm, orbital),
+                (kernel_hbm, kernel),
+                (flips_hbm, flips),
+                (row_hbm, row_flip),
+                (partners_hbm, partners),
+                (corners_hbm, corners),
+                (twiddle_hbm, twiddle_ref),
+                (edge_hbm, edge_table),
+                (plane_hbm, plane_table),
+            ]
+        )
+    ]
+    for load in loads:
+        load.start()
     barrier = pltpu.get_barrier_semaphore()
     for t, u, v in reached:
         pl.semaphore_signal(
@@ -198,6 +225,7 @@
             device_id=place({"slab": t, "orb": u, "rep": v}),
             device_id_type=MESH,
         )
+    loads[0].wait()
     pl.semaphore_wait(barrier, len(reached))
 
     def slot_of(t, u):
@@ -221,10 +249,10 @@
 
     centre = orbital[0].astype(jnp.float32)
     boxes[slot_of(0, 0)] = orbital[0]
+    for load in loads[1:4]:
+        load.wait()
     for n, chunk in enumerate(prepared_kernel(kernel[...], flips, row_flip[...], edge)):
         spectrum[n] = chunk
-    twiddle = twiddle_ref[...]
-    edge_tab = edge_table[...]
 
     forwards = []
     for t, u in box_moves:
@@ -248,7 +276,10 @@
             )
             copy.start()
             forwards.append(copy)
-    table_copy.wait()
+    for load in loads[4:]:
+        load.wait()
+    twiddle = twiddle_ref[...]
+    edge_tab = edge_table[...]
     for copy in forwards:
         copy.wait()
 
@@ -263,7 +294,7 @@
         known = jnp.maximum(partner, 0)
         offsets = []
         for axis, length in enumerate(lengths):
-            delta = corners[own_row, axis] - corners[known, axis]
+            delta = corners[axis, own_row] - corners[axis, known]
             delta = jnp.where(delta < -(length // 2), delta + length, delta)
             delta = jnp.where(delta >= length - length // 2, delta - length, delta)
             offsets.append(delta)
@@ -280,7 +311,40 @@
         inside = (from_b >= 0) & (from_b < edge) & (from_c >= 0) & (from_c < edge)
         return jnp.where(inside_a & inside, box, 0.0)
 
+    def start_stage(stage, tile):
+        me = number_of(stage, {})
+        energies[stage, me] = tile
+        copies = []
+        for n, m in enumerate(stage_moves[stage]):
+            copies.append(
+                pltpu.make_async_remote_copy(
+                    src_ref=energies.at[stage, me],
+                    dst_ref=energies.at[stage, me],
+                    send_sem=energy_send.at[stage, n],
+                    recv_sem=energy_recv.at[stage, n],
+                    device_id=place(m),
+                    device_id_type=MESH,
+                )
+            )
+            copies[-1].start()
+        return copies
+
+    def finish_stage(stage, copies):
+        for copy in copies:
+            copy.wait()
+        result = energies[stage, 0]
+        for n in range(1, math.prod(sizes[a] for a in stages[stage])):
+            result = result + energies[stage, n]
+        return result
+
+    def number_of(stage, moved):
+        result = 0
+        for a in stages[stage]:
+            result = result * sizes[a] + moved.get(a, here[a])
+        return result
+
     part = plane // RADIX
+    weighed = jnp.zeros((edge, part), jnp.float32)
     cuts = [slice(n * part, (n + 1) * part) for n in range(RADIX)]
     total = jnp.zeros((edge, plane), jnp.float32)
     for start in range(0, slot_count, 2 * FIELDS):
@@ -296,7 +360,15 @@
         for n, block in enumerate(blocks):
             re, im = edge_turn(block, edge_tab)
             factor = spectrum[n % RADIX]
-            blocks[n] = edge_turn((re * factor, -im * factor), edge_tab)
+            blocks[n] = (re * factor, -im * factor)
+            weighed = weighed + (re * blocks[n][0] - im * blocks[n][1])
+        if start + 2 * FIELDS >= slot_count:
+            tile = weighed[:, :128]
+            for n in range(128, part, 128):
+                tile = tile + weighed[:, n : n + 128]
+            tile = sum(tile[n : n + 8] for n in range(8, edge, 8)) + tile[:8]
+            copies = start_stage(0, tile)
+        blocks = [edge_turn(block, edge_tab) for block in blocks]
         blocks = plane_turn(blocks, plane_table[...])
         for n in range(0, len(moved), 2):
             field = blocks[n // 2 * RADIX : (n // 2 + 1) * RADIX]
@@ -305,12 +377,6 @@
             re, im = jnp.concatenate(re, axis=1), jnp.concatenate(im, axis=1)
             total = total + (im * moved[n + 1] - re * moved[n])
     mine[0] = total
-    weighed = centre * total
-    tile = weighed[:, :128]
-    for n in range(128, plane, 128):
-        tile = tile + weighed[:, n : n + 128]
-    tile = sum(tile[n : n + 8] for n in range(8, edge, 8)) + tile[:8]
-
     swaps = []
     for v in range(1, reps):
         copy = pltpu.make_async_remote_copy(
@@ -324,42 +390,22 @@
         copy.start()
         swaps.append(copy)
 
-    for stage, (axes, moves) in enumerate(zip(stages, stage_moves)):
-        count = math.prod(sizes[a] for a in axes)
-
-        def number(moved):
-            result = 0
-            for a in axes:
-                result = result * sizes[a] + moved.get(a, here[a])
-            return result
-
-        me = number({})
-        energies[stage, me] = tile
-        copies = []
-        for n, m in enumerate(moves):
-            copies.append(
-                pltpu.make_async_remote_copy(
-                    src_ref=energies.at[stage, me],
-                    dst_ref=energies.at[stage, me],
-                    send_sem=energy_send.at[stage, n],
-                    recv_sem=energy_recv.at[stage, n],
-                    device_id=place(m),
-                    device_id_type=MESH,
-                )
-            )
-            copies[-1].start()
-        for copy in copies:
-            copy.wait()
-        tile = energies[stage, 0]
-        for n in range(1, count):
-            tile = tile + energies[stage, n]
-    orbital_total = slabs * orbs
-    value = jnp.sum(tile, keepdims=True) * (1.0 / (2.0 * orbital_total * edge**3))
-    energy_out[...] = jnp.broadcast_to(value, energy_out.shape)
+    tile = finish_stage(0, copies)
+    for stage in range(1, len(stages)):
+        tile = finish_stage(stage, start_stage(stage, tile))
+    energy_out[...] = tile
     for copy in swaps:
         copy.wait()
     for _, copy in sends:
         copy.wait_send()
+
+
+def finished(scale, reps, mine, theirs, energy, result, total):
+    value = mine[0]
+    for v in range(reps - 1):
+        value = value + theirs[v]
+    result[0] = value
+    total[0] = jnp.sum(energy[...]) * scale
 
 
 def body(orbitals, corners, partners, kernel):
@@ -382,7 +428,6 @@
     edge_stack, plane_stack, twiddle, flips, row_flip = tables(edge)
     count = len(steps) * orbs
     vmem = pl.BlockSpec(memory_space=pltpu.VMEM)
-    smem = pl.BlockSpec(memory_space=pltpu.SMEM)
     dma = pltpu.SemaphoreType.DMA
     mine, theirs, energy = pl.pallas_call(
         functools.partial(fused, cfg),
@@ -391,14 +436,22 @@
             jax.ShapeDtypeStruct((max(reps - 1, 1), edge, plane), jnp.float32),
             jax.ShapeDtypeStruct((8, 128), jnp.float32),
         ),
-        in_specs=[smem, smem, vmem, vmem, vmem, pl.BlockSpec(memory_space=pl.ANY), vmem, vmem, vmem],
+        in_specs=[pl.BlockSpec(memory_space=pl.ANY)] * 9,
         out_specs=(vmem, vmem, vmem),
         scratch_shapes=[
+            pltpu.SMEM(partners.shape, jnp.int32),
+            pltpu.SMEM(corners.shape[::-1], jnp.int32),
+            pltpu.VMEM(orbitals.shape, jnp.bfloat16),
+            pltpu.VMEM(kernel.shape, jnp.float32),
+            pltpu.VMEM(edge_stack.shape, jnp.bfloat16),
+            pltpu.VMEM(twiddle.shape, jnp.float32),
+            pltpu.VMEM(flips.shape, jnp.bfloat16),
+            pltpu.VMEM(row_flip.shape, jnp.bfloat16),
             pltpu.VMEM((count, edge, plane), jnp.bfloat16),
             pltpu.VMEM(plane_stack.shape, jnp.bfloat16),
             pltpu.VMEM((RADIX, edge, plane // RADIX), jnp.float32),
             pltpu.VMEM((len(stages), widest, 8, 128), jnp.float32),
-            dma,
+            dma((9,)),
             dma((count,)),
             dma((count,)),
             dma((count, reps)),
@@ -411,7 +464,7 @@
         compiler_params=pltpu.CompilerParams(collective_id=0, has_side_effects=True),
     )(
         partners,
-        corners,
+        corners.T,
         orbitals,
         kernel,
         jnp.asarray(edge_stack),
@@ -420,10 +473,16 @@
         jnp.asarray(flips),
         jnp.asarray(row_flip),
     )
-    result = mine
-    for v in range(reps - 1):
-        result = result + theirs[v : v + 1]
-    return result, energy[0, :1]
+    scale = -1.0 / (2.0 * slabs * orbs * edge**3)
+    return pl.pallas_call(
+        functools.partial(finished, scale, reps),
+        out_shape=(
+            jax.ShapeDtypeStruct((1, edge, plane), jnp.float32),
+            jax.ShapeDtypeStruct((1,), jnp.float32),
+        ),
+        in_specs=[vmem] * 3,
+        out_specs=(vmem, pl.BlockSpec(memory_space=pltpu.SMEM)),
+    )(mine, theirs, energy)
 
 
 def solution(mesh):

time: 29 us -> 24.5 us (0.84)
  local copies, waits for them, and re-layouts: 2.54 us -> 0 us
  other arithmetic: 1.64 us -> 0 us
    pallas_call x1, Pallas kernels: 23.9 us -> 22.1 us  [body(): pl.pallas_call(functools.partial(fused, cfg), out_shape=(jax.ShapeDtypeSt...]
    pallas_call x0 -> x1, Pallas kernels: none -> 1.65 us  [body(): pl.pallas_call(functools.partial(finished, scale, reps), out_shape=(jax.S...]
    add x1 -> x0, other arithmetic: 1.64 us -> none  [body(): result = result + theirs[v:v + 1]]
    unnamed x1 -> x0, local copies, waits for them, and re-layouts: 1.35 us -> none
    slice x1 -> x0, local copies, waits for them, and re-layouts: 1.2 us -> none  [body(): return (result, energy[0, :1])]
where the time goes in v2:
time: 24.5 us; the launch traced here: 24.4 us
  Pallas kernels  23.8 us (97%)
  between operations  0.64 us (3%)
    pallas_call x1, Pallas kernels, body(): pl.pallas_call(functools.partial(fused, cfg), out_shape=(jax.ShapeDtypeSt...  22.1 us
    pallas_call x1, Pallas kernels, body(): pl.pallas_call(functools.partial(finished, scale, reps), out_shape=(jax.S...  1.65 us

profile of v2, /device:TPU:0, one launch (start us, length us, event | category | flops | bytes accessed | tf_op | source)
XLA Modules:
  0.0 24.4 jit_solution(7932667534593561962)
XLA Ops:
  0.6 22.1 %shard_map.104 = (f32[1,32,1024]{2,1,0:T(8,128)}, f32[1,32,1024]{2,1,0:T(8,128)}, f32[8,128]{1,0:T(8,128)}) custom-call(s32[1,24]{1,0:T(1,128)} %refs_0_.1, s32[3,8]{1,0:T(4,128)} %bitcast.1, bf16[1,32,1024]{2,1,0:T(8,128)(2,1)} %refs_2_.1, f32[32,1024]{1,0:T(8,128)} %refs_3_.1, bf16[64,192]{1,0:T(8,128)(2,1)} %constant.10.clone.refs_4_, ...), custom_call_target="tpu_custom_call" | custom-call | tf_op jit(solution)/shard_map/pallas_call | solution.py:432
  22.7 1.7 %shard_map.105 = (f32[1,32,1024]{2,1,0:T(8,128)}, f32[1]{0:T(128)}) custom-call(f32[1,32,1024]{2,1,0:T(8,128)} %get-tuple-element.5.mine, f32[1,32,1024]{2,1,0:T(8,128)} %get-tuple-element.6.theirs, f32[8,128]{1,0:T(8,128)} %get-tuple-element.7.energy), custom_call_target="tpu_custom_call" | custom-call | tf_op jit(solution)/shard_map/pallas_call | solution.py:477

commit v3 on v2

--- a/solution.py
+++ b/solution.py
@@ -234,18 +234,34 @@
     cut = edge // reps
     share = pl.ds(pl.multiple_of(rep * cut, cut), cut)
     sends = []
-    for t, u in box_moves:
-        target = slot_of(-t, -u)
+
+    def send(source, target, send_sem, move):
         copy = pltpu.make_async_remote_copy(
-            src_ref=orbital.at[0, share],
+            src_ref=orbital.at[0, share] if source is None else boxes.at[source, share],
             dst_ref=boxes.at[target, share],
-            send_sem=box_send.at[target],
+            send_sem=send_sem,
             recv_sem=box_recv.at[target],
-            device_id=place({"slab": t, "orb": u}),
+            device_id=move,
             device_id_type=MESH,
         )
         copy.start()
-        sends.append((slot_of(t, u), copy))
+        sends.append(copy)
+
+    low = slab < slabs // 2
+    moves = [t for t in steps if t % slabs]
+    ordered = [
+        jnp.where(low, after, before) if shift_back == 0 else after
+        for before, after in zip(moves, reversed(moves))
+    ]
+
+    def slot_at(t, u=0):
+        return lax.rem(t + shift_back + slabs, slabs) * orbs + u % orbs
+
+    for u in range(1, orbs):
+        send(None, slot_of(0, -u), box_send.at[slot_of(0, -u)], place({"orb": u}))
+    for t in ordered:
+        target = slot_at(-t)
+        send(None, target, box_send.at[target], {"slab": lax.rem(slab + t + slabs, slabs)})
 
     centre = orbital[0].astype(jnp.float32)
     boxes[slot_of(0, 0)] = orbital[0]
@@ -255,16 +271,18 @@
         spectrum[n] = chunk
 
     forwards = []
-    for t, u in box_moves:
-        slot = slot_of(t, u)
+
+    def arrived(slot):
         pltpu.make_async_remote_copy(
             src_ref=orbital.at[0, share],
             dst_ref=boxes.at[slot, share],
             send_sem=box_send.at[slot],
             recv_sem=box_recv.at[slot],
-            device_id=place({"slab": t, "orb": u}),
+            device_id=place({"rep": 1}),
             device_id_type=MESH,
         ).wait_recv()
+
+    def share_box(slot):
         for v in range(1, reps):
             copy = pltpu.make_async_remote_copy(
                 src_ref=boxes.at[slot, share],
@@ -276,6 +294,17 @@
             )
             copy.start()
             forwards.append(copy)
+
+    for t in reversed(ordered):
+        arrived(slot_at(t))
+        for u in range(1, orbs):
+            target = slot_at(t, -u)
+            send(slot_at(t), target, box_send.at[target], place({"orb": u}))
+        share_box(slot_at(t))
+    for u in range(1, orbs):
+        for slot in [slot_of(0, u), *[slot_at(t, u) for t in reversed(ordered)]]:
+            arrived(slot)
+            share_box(slot)
     for load in loads[4:]:
         load.wait()
     twiddle = twiddle_ref[...]
@@ -396,7 +425,7 @@
     energy_out[...] = tile
     for copy in swaps:
         copy.wait()
-    for _, copy in sends:
+    for copy in sends:
         copy.wait_send()
 
 

time: 24.5 us -> 24.2 us (0.988)
  Pallas kernels: 23.8 us -> 23.4 us
    pallas_call x1, Pallas kernels: 22.1 us -> 21.7 us  [body(): pl.pallas_call(functools.partial(fused, cfg), out_shape=(jax.ShapeDtypeSt...]
where the time goes in v3:
time: 24.2 us; the launch traced here: 24 us
  Pallas kernels  23.4 us (97%)
  between operations  0.64 us (3%)
    pallas_call x1, Pallas kernels, body(): pl.pallas_call(functools.partial(fused, cfg), out_shape=(jax.ShapeDtypeSt...  21.7 us
    pallas_call x1, Pallas kernels, body(): pl.pallas_call(functools.partial(finished, scale, reps), out_shape=(jax.S...  1.65 us

profile of v3, /device:TPU:0, one launch (start us, length us, event | category | flops | bytes accessed | tf_op | source)
XLA Modules:
  0.0 24.0 jit_solution(10664822984831950590)
XLA Ops:
  0.6 21.7 %shard_map.104 = (f32[1,32,1024]{2,1,0:T(8,128)}, f32[1,32,1024]{2,1,0:T(8,128)}, f32[8,128]{1,0:T(8,128)}) custom-call(s32[1,24]{1,0:T(1,128)} %refs_0_.1, s32[3,8]{1,0:T(4,128)} %bitcast.1, bf16[1,32,1024]{2,1,0:T(8,128)(2,1)} %refs_2_.1, f32[32,1024]{1,0:T(8,128)} %refs_3_.1, bf16[64,192]{1,0:T(8,128)(2,1)} %constant.10.clone.refs_4_, ...), custom_call_target="tpu_custom_call" | custom-call | tf_op jit(solution)/shard_map/pallas_call | solution.py:461
  22.4 1.7 %shard_map.105 = (f32[1,32,1024]{2,1,0:T(8,128)}, f32[1]{0:T(128)}) custom-call(f32[1,32,1024]{2,1,0:T(8,128)} %get-tuple-element.5.mine, f32[1,32,1024]{2,1,0:T(8,128)} %get-tuple-element.6.theirs, f32[8,128]{1,0:T(8,128)} %get-tuple-element.7.energy), custom_call_target="tpu_custom_call" | custom-call | tf_op jit(solution)/shard_map/pallas_call | solution.py:506
